TPU v7x, 32 devices: a whole 2x2x4 slice. The times are simulated.
32 devices in a mesh: row: 8 (over z, y), col: 4 (over x, core).
Axes of the slice: x: 2, y: 2, z: 4, core: 2. Of those that a mesh axis runs over, the one named last changes fastest.
Arguments:
- matrix: float32 [4096, 4096], P('row', 'col'), may hold values from -0.92 to 1.92, as said below
Outputs:
- inverse: float32 [4096, 4096], P('row', 'col')
- residual_norms: float32 [4], replicated
Inputs may be any that keep to these rules, and one draw needn't show every extreme that they name: matrix is exactly symmetric and positive definite; all its eigenvalues lie between 0.08 and 1.92.
All inputs are finite; a program needn't handle non-finite values.
Results may differ from a plain program's by a relative error of at most 0.0017.
The roundings to bfloat16 on the way count: a program that leaves them out, or rounds other values in their place, can miss the bound.
Values may be sent and summed in bfloat16 or wider, within the bound.
A program may use at most 64 MiB of HBM per device.

v0:
```python
import jax
import jax.numpy as jnp
from jax import lax
from jax.sharding import PartitionSpec as P

ITERS = 4


def rounded(value):
    return lax.reduce_precision(value, 8, 7)


def first_iterate(panel, scale_low, row_start, col_start):
    rows = row_start + lax.broadcasted_iota(jnp.int32, panel.shape, 0)
    cols = col_start + lax.broadcasted_iota(jnp.int32, panel.shape, 1)
    eye = (rows == cols).astype(jnp.float32)
    shift = rounded(eye + (eye - scale_low * panel.astype(jnp.float32)))
    return (scale_low * shift).astype(jnp.bfloat16)


def transpose_blocks(block, row_size, col_size):
    ratio = row_size // col_size
    side = block.shape[0]
    row_index = lax.axis_index("row")
    pieces = []
    for turn in range(ratio):
        pairs = []
        for row in range(row_size):
            for col in range(col_size):
                target_row = ratio * col + (row + turn) % ratio
                pairs.append((row * col_size + col, target_row * col_size + row // ratio))
        half = lax.rem(row_index + turn, ratio)
        piece = lax.dynamic_slice_in_dim(block, half * side, side, axis=1)
        pieces.append(lax.ppermute(piece, ("row", "col"), pairs).T)
    out = jnp.zeros_like(block)
    for turn in range(ratio):
        half = lax.rem(row_index - turn + ratio, ratio)
        out = lax.dynamic_update_slice_in_dim(out, pieces[turn], half * side, axis=1)
    return out


def shards(matrix):
    row_count, col_count = matrix.shape
    row_size, col_size = (lax.axis_size("row"), lax.axis_size("col"))
    order = col_count * col_size
    row_start = lax.axis_index("row") * row_count
    col_start = lax.axis_index("col") * col_count
    global_rows = row_start + lax.broadcasted_iota(jnp.int32, (row_count, col_count), 0)
    global_cols = col_start + lax.broadcasted_iota(jnp.int32, (row_count, col_count), 1)
    eye_block = (global_rows == global_cols).astype(jnp.float32)
    mat_low = matrix.astype(jnp.bfloat16)
    sq_total = lax.psum(jnp.sum(matrix * matrix), ("row", "col"))
    panel_rows = lax.all_gather(mat_low, "col", axis=1, tiled=True)
    panel_cols = lax.all_gather(mat_low, "row", axis=0, tiled=True)
    start_scale = jnp.sqrt(jnp.float32(order)) / jnp.sqrt(sq_total)
    scale_low = rounded(start_scale)
    residual = eye_block - scale_low * rounded(matrix)
    partial_list = [jnp.sum(residual * residual)]
    iterate_rows = first_iterate(panel_rows, scale_low, row_start, 0)
    iterate_cols = first_iterate(panel_cols, scale_low, 0, col_start)
    for iteration in range(1, ITERS):
        product = jnp.dot(iterate_rows, panel_cols, preferred_element_type=jnp.float32)
        residual = eye_block - product
        partial_list.append(jnp.sum(residual * residual))
        shift_low = (eye_block + residual).astype(jnp.bfloat16)
        current = jnp.dot(
            lax.all_gather(shift_low, "col", axis=1, tiled=True),
            iterate_cols,
            preferred_element_type=jnp.float32,
        )
        if iteration < ITERS - 1:
            cur_low = current.astype(jnp.bfloat16)
            iterate_rows = lax.all_gather(cur_low, "col", axis=1, tiled=True)
            iterate_cols = lax.all_gather(cur_low, "row", axis=0, tiled=True)
    summed = lax.psum(jnp.stack(partial_list), ("row", "col"))
    residual_norms = jnp.sqrt(summed / order)
    return (transpose_blocks(current, row_size, col_size), residual_norms)


def solution(mesh):
    in_specs = (P("row", "col"),)
    out_specs = (P("row", "col"), P())
    return jax.shard_map(shards, mesh=mesh, in_specs=in_specs, out_specs=out_specs, check_vma=False)
```

profile of v0, /device:TPU:0, one launch (start us, length us, event | category | flops | bytes accessed | tf_op | source)
XLA Modules:
  0.0 790.7 jit_solution(10998236796299218012)
XLA Ops:
  7.2 0.0 all-gather.10.cloned.1.call-start
  7.2 4.3 multiply_reduce_fusion.3
  11.5 0.0 all-gather.10.cloned.1.call-update
  11.5 0.0 all-gather.12.cloned.1.call-start
  11.5 0.7 all-gather.12.cloned.1.call-update
  12.3 0.0 all-gather.14.cloned.1.call-start
  12.3 42.5 %psum.14 = f32[]{:T(128)} all-reduce(f32[]{:T(128)} %get-tuple-element.9), channel_id=1, replica_groups=mesh['row'=8,'col'=4] {'row','col'}, use_global_device_ids=true, to_apply=%region_1.0 | all-reduce | flops 1 | bytes 8 | tf_op jit(solution)/shard_map/psum | solution.py:52
  56.0 120.3 %all-gather.12.cloned.1.call-done = bf16[4096,1024]{1,0:T(8,128)(2,1)} async-done(((bf16[512,1024]{1,0:T(8,128)(2,1)}), bf16[4096,1024]{1,0:T(8,128)(2,1)}) %all-gather.12.cloned.1.call-update) | async-done | bytes 8388624 | tf_op jit(solution)/shard_map/all_gather | solution.py:54
  176.3 12.1 %fusion.12 = (bf16[512,1024]{1,0:T(8,128)(2,1)}, f32[512,1024]{1,0:T(8,128)}) fusion(s32[1024]{0:T(1024)S(1)} %iota_add_fusion, s32[512]{0:T(512)S(1)} %iota_add_fusion.1, bf16[4096,1024]{1,0:T(8,128)(2,1)} %all-gather.12.cloned.1.call-done, bf16[512,4096]{1,0:T(8,128)(2,1)} %all-gather.10.cloned.1.call-done, f32[]{:T(128)} %reduce_precision.12), kind=kOutput, calls=%fused_computation.21 | convolution fusion | flops 4316463104 | bytes 15734788 | tf_op jit(solution)/shard_map/dot_general | solution.py:62
  188.4 0.0 all-gather.14.cloned.1.call-update
  188.5 0.0 all-gather.16.cloned.1.call-start
  188.5 32.7 %all-gather.14.cloned.1.call-done = bf16[512,4096]{1,0:T(8,128)(2,1)} async-done(((bf16[512,1024]{1,0:T(8,128)(2,1)}), bf16[512,4096]{1,0:T(8,128)(2,1)}) %all-gather.14.cloned.1.call-update) | async-done | bytes 4194320 | tf_op jit(solution)/shard_map/all_gather | solution.py:67
  221.3 12.0 %fusion.17 = bf16[512,1024]{1,0:T(8,128)(2,1)} fusion(bf16[512,4096]{1,0:T(8,128)(2,1)} %all-gather.14.cloned.1.call-done, bf16[4096,1024]{1,0:T(8,128)(2,1)} %all-gather.12.cloned.1.call-done, s32[1024]{0:T(1024)S(1)} %iota_add_fusion, f32[]{:T(128)} %reduce_precision.12), kind=kOutput, calls=%fused_computation.30 | convolution fusion | flops 4333240320 | bytes 13635588 | tf_op jit(solution)/shard_map/dot_general | solution.py:66
  233.2 0.0 all-gather.16.cloned.1.call-update
  233.3 0.2 all-gather.18.cloned.1.call-start
  233.5 34.4 %all-gather.16.cloned.1.call-done = bf16[512,4096]{1,0:T(8,128)(2,1)} async-done(((bf16[512,1024]{1,0:T(8,128)(2,1)}), bf16[512,4096]{1,0:T(8,128)(2,1)}) %all-gather.16.cloned.1.call-update) | async-done | bytes 4194320 | tf_op jit(solution)/shard_map/all_gather | solution.py:73
  267.9 10.9 %fusion.13 = (bf16[512,1024]{1,0:T(8,128)(2,1)}, f32[512,1024]{1,0:T(8,128)}) fusion(s32[1024]{0:T(1024)S(1)} %iota_add_fusion, s32[512]{0:T(512)S(1)} %iota_add_fusion.1, bf16[512,4096]{1,0:T(8,128)(2,1)} %all-gather.16.cloned.1.call-done, bf16[4096,1024]{1,0:T(8,128)(2,1)} %all-gather.12.cloned.1.call-done), kind=kOutput, calls=%fused_computation.22 | convolution fusion | flops 4297588736 | bytes 15734784 | tf_op jit(solution)/shard_map/dot_general | solution.py:62
  278.7 0.0 all-gather.18.cloned.1.call-update
  278.8 0.0 all-gather.20.cloned.1.call-start
  278.8 0.5 all-gather.20.cloned.1.call-update
  279.3 0.0 copy-start.1
  279.4 0.0 all-gather.22.cloned.1.call-start
  279.4 34.0 %all-gather.18.cloned.1.call-done = bf16[512,4096]{1,0:T(8,128)(2,1)} async-done(((bf16[512,1024]{1,0:T(8,128)(2,1)}), bf16[512,4096]{1,0:T(8,128)(2,1)}) %all-gather.18.cloned.1.call-update) | async-done | bytes 4194320 | tf_op jit(solution)/shard_map/all_gather | solution.py:67
  313.4 126.5 %all-gather.20.cloned.1.call-done = bf16[4096,1024]{1,0:T(8,128)(2,1)} async-done(((bf16[512,1024]{1,0:T(8,128)(2,1)}), bf16[4096,1024]{1,0:T(8,128)(2,1)}) %all-gather.20.cloned.1.call-update) | async-done | bytes 8388624 | tf_op jit(solution)/shard_map/all_gather | solution.py:74
  439.9 10.2 %convolution_convert_fusion = bf16[512,1024]{1,0:T(8,128)(2,1)} fusion(bf16[512,4096]{1,0:T(8,128)(2,1)} %all-gather.18.cloned.1.call-done, bf16[4096,1024]{1,0:T(8,128)(2,1)} %all-gather.20.cloned.1.call-done), kind=kOutput, calls=%fused_computation.31 | convolution fusion | flops 4295491584 | bytes 13631488 | tf_op jit(solution)/shard_map/dot_general | solution.py:66
  450.0 0.0 all-gather.22.cloned.1.call-update
  450.1 0.0 all-gather.24.cloned.1.call-start
  450.1 32.7 %all-gather.22.cloned.1.call-done = bf16[512,4096]{1,0:T(8,128)(2,1)} async-done(((bf16[512,1024]{1,0:T(8,128)(2,1)}), bf16[512,4096]{1,0:T(8,128)(2,1)}) %all-gather.22.cloned.1.call-update) | async-done | bytes 4194320 | tf_op jit(solution)/shard_map/all_gather | solution.py:73
  482.8 13.2 %fusion.16 = (f32[]{:T(128)}, f32[]{:T(128)}, f32[]{:T(128)}, f32[]{:T(128)}, bf16[512,1024]{1,0:T(8,128)(2,1)}) fusion(f32[512,1024]{1,0:T(8,128)S(1)} %copy-done.1, f32[]{:T(128)} %reduce_precision.12, s32[1024]{0:T(1024)S(1)} %iota_add_fusion, s32[512]{0:T(512)S(1)} %iota_add_fusion.1, f32[512,1024]{1,0:T(8,128)} %get-tuple-element.14, ...), kind=kOutput, calls=%fused_computation.25 | convolution fusion | flops 4304404480 | bytes 19929108 | tf_op jit(solution)/shard_map/dot_general | solution.py:62
  496.0 0.0 all-gather.24.cloned.1.call-update
  496.0 0.3 all-gather.26.cloned.1.call-start
  496.3 0.5 all-gather.26.cloned.1.call-update
  496.8 33.9 %all-gather.24.cloned.1.call-done = bf16[512,4096]{1,0:T(8,128)(2,1)} async-done(((bf16[512,1024]{1,0:T(8,128)(2,1)}), bf16[512,4096]{1,0:T(8,128)(2,1)}) %all-gather.24.cloned.1.call-update) | async-done | bytes 4194320 | tf_op jit(solution)/shard_map/all_gather | solution.py:67
  530.6 126.6 %all-gather.26.cloned.1.call-done = bf16[4096,1024]{1,0:T(8,128)(2,1)} async-done(((bf16[512,1024]{1,0:T(8,128)(2,1)}), bf16[4096,1024]{1,0:T(8,128)(2,1)}) %all-gather.26.cloned.1.call-update) | async-done | bytes 8388624 | tf_op jit(solution)/shard_map/all_gather | solution.py:74
  657.3 8.1 %fusion.20 = f32[512,1024]{1,0:T(8,128)S(1)} fusion(bf16[512,4096]{1,0:T(8,128)(2,1)} %all-gather.24.cloned.1.call-done, bf16[4096,1024]{1,0:T(8,128)(2,1)} %all-gather.26.cloned.1.call-done), kind=kOutput, calls=%fused_computation.40 | convolution fusion | flops 4294967296 | bytes 14680064 | tf_op jit(solution)/shard_map/dot_general | solution.py:66
  665.4 0.2 constant_dynamic-slice_fusion
  665.7 1.6 collective-permute-start
  667.3 0.6 collective-permute-start.1
  667.8 2.5 pad_maximum_fusion
  670.4 109.5 %psum.15 = f32[4]{0:T(128)S(1)} all-reduce(f32[4]{0:T(128)S(1)} %pad_maximum_fusion), channel_id=1, replica_groups=mesh['row'=8,'col'=4] {'row','col'}, use_global_device_ids=true, to_apply=%region_6.0 | all-reduce | flops 4 | bytes 32 | tf_op jit(solution)/shard_map/psum | solution.py:75
  779.9 0.5 multiply_sqrt_fusion
  780.4 1.6 copy.3
  782.0 0.3 copy.4
  782.4 0.2 broadcast_in_dim.3
  782.6 0.1 constant_dynamic-update-slice_fusion.1
  782.7 0.1 constant_dynamic-update-slice_fusion
  782.8 0.0 copy-start
  782.8 1.3 copy-done
  (6 shorter events, 0.0 us)
Async XLA Ops:
  7.2 48.9 %all-gather.10.cloned.1.call-start = ((), (), s32[]{:S(2)}) async-start(), calls=%async_computation | async-start | bytes 5242880 | tf_op jit(solution)/shard_map/all_gather | solution.py:53
  11.5 164.8 %all-gather.12.cloned.1.call-start = ((), (), s32[]{:S(2)}) async-start(), calls=%async_computation.1 | async-start | bytes 9437184 | tf_op jit(solution)/shard_map/all_gather | solution.py:54
  12.3 209.0 %all-gather.14.cloned.1.call-start = ((), (), s32[]{:S(2)}) async-start(), calls=%async_computation.2 | async-start | bytes 5242880 | tf_op jit(solution)/shard_map/all_gather | solution.py:67
  188.5 79.4 %all-gather.16.cloned.1.call-start = ((), (), s32[]{:S(2)}) async-start(), calls=%async_computation.3 | async-start | bytes 5242880 | tf_op jit(solution)/shard_map/all_gather | solution.py:73
  233.3 80.1 %all-gather.18.cloned.1.call-start = ((), (), s32[]{:S(2)}) async-start(), calls=%async_computation.4 | async-start | bytes 5242880 | tf_op jit(solution)/shard_map/all_gather | solution.py:67
  278.8 161.1 %all-gather.20.cloned.1.call-start = ((), (), s32[]{:S(2)}) async-start(), calls=%async_computation.5 | async-start | bytes 9437184 | tf_op jit(solution)/shard_map/all_gather | solution.py:74
  279.3 203.5 %copy-start.1 = (f32[512,1024]{1,0:T(8,128)S(1)}, f32[512,1024]{1,0:T(8,128)}, u32[]{:S(2)}) copy-start(f32[512,1024]{1,0:T(8,128)} %param.1) | copy-start | bytes 6291460
  279.4 203.5 %all-gather.22.cloned.1.call-start = ((), (), s32[]{:S(2)}) async-start(), calls=%async_computation.6 | async-start | bytes 5242880 | tf_op jit(solution)/shard_map/all_gather | solution.py:73
  450.1 80.6 %all-gather.24.cloned.1.call-start = ((), (), s32[]{:S(2)}) async-start(), calls=%async_computation.7 | async-start | bytes 5242880 | tf_op jit(solution)/shard_map/all_gather | solution.py:67
  496.0 161.3 %all-gather.26.cloned.1.call-start = ((), (), s32[]{:S(2)}) async-start(), calls=%async_computation.8 | async-start | bytes 9437184 | tf_op jit(solution)/shard_map/all_gather | solution.py:74
  665.7 114.8 %collective-permute-start = (f32[512,512]{1,0:T(8,128)S(1)}, f32[512,512]{1,0:T(8,128)}, u32[]{:S(2)}, u32[]{:S(2)}) collective-permute-start(f32[512,512]{1,0:T(8,128)S(1)} %get-tuple-element.8), channel_id=1, source_target_pairs={{0,0},{1,8},{2,16},{3,24},{4,4},{5,12},{6,20},{7,28},{8,1},{9,9},{... | collective-permute-start | bytes 3145736 | tf_op jit(solution)/shard_map/ppermute | solution.py:34
  667.3 114.7 %collective-permute-start.1 = (f32[512,512]{1,0:T(8,128)S(1)}, f32[512,512]{1,0:T(8,128)S(1)}, u32[]{:S(2)}, u32[]{:S(2)}) collective-permute-start(f32[512,512]{1,0:T(8,128)S(1)} %get-tuple-element.7), channel_id=1, source_target_pairs={{0,4},{1,12},{2,20},{3,28},{4,0},{5,8},{6,16},{7,24},{8,5},{9,13},... | collective-permute-start | bytes 3145736 | tf_op jit(solution)/shard_map/ppermute | solution.py:34
  782.8 1.3 copy-start
Sparse Core Ops, SparseCore 0:
  11.6 37.4 all-gather.9
  51.8 124.4 all-gather.11
  188.6 32.6 all-gather.13
  233.4 34.4 all-gather.15
  278.9 34.4 all-gather.17
  315.4 124.4 all-gather.19
  450.2 32.6 all-gather.21
  496.1 34.4 all-gather.23
  532.8 124.4 all-gather.25
where the time goes:
time: 791 us
  waiting for transfers between devices  543 us (69%)
  blocking collectives  152 us (19%)
  matrix products  66.4 us (8%)
  between operations  15.1 us (2%)
    all_gather x2, waiting for transfers between devices, shards(): iterate_cols = lax.all_gather(cur_low, 'row', axis=0, tiled=True)  253 us
    all_gather x1, waiting for transfers between devices, shards(): panel_cols = lax.all_gather(mat_low, 'row', axis=0, tiled=True)  120 us
    psum x1, blocking collectives, shards(): summed = lax.psum(jnp.stack(partial_list), ('row', 'col'))  110 us
    all_gather x3, waiting for transfers between devices, shards(): lax.all_gather(shift_low, 'col', axis=1, tiled=True)  101 us
    all_gather x2, waiting for transfers between devices, shards(): iterate_rows = lax.all_gather(cur_low, 'col', axis=1, tiled=True)  67.1 us
    psum x1, blocking collectives, shards(): sq_total = lax.psum(jnp.sum(matrix * matrix), ('row', 'col'))  42.5 us
    dot_general x3, matrix products, shards(): jnp.dot(iterate_rows, panel_cols, preferred_element_type=jnp.float32)  36.2 us
    dot_general x3, matrix products, shards(): jnp.dot(lax.all_gather(shift_low, 'col', axis=1, tiled=True), iterate_col...  30.3 us
  transfers between devices with their start and end apart: 11, of which 8 were waited for; matrix products, arithmetic and copies ran while one was open for 1% of the time, Pallas kernels for 0%

commit v1 on v0

--- a/solution.py
+++ b/solution.py
@@ -72,7 +72,7 @@
             cur_low = current.astype(jnp.bfloat16)
             iterate_rows = lax.all_gather(cur_low, "col", axis=1, tiled=True)
             iterate_cols = lax.all_gather(cur_low, "row", axis=0, tiled=True)
-    summed = lax.psum(jnp.stack(partial_list), ("row", "col"))
+    summed = lax.psum(lax.psum(jnp.stack(partial_list), "col"), "row")
     residual_norms = jnp.sqrt(summed / order)
     return (transpose_blocks(current, row_size, col_size), residual_norms)
 

time: 791 us -> 778 us (0.984)
  the two profiles are of different devices: /device:TPU:0 before, /device:TPU:8 now
where the time goes in v1:
time: 778 us
  waiting for transfers between devices  541 us (70%)
  blocking collectives  139 us (18%)
  matrix products  66.4 us (9%)
  between operations  15.2 us (2%)
    all_gather x2, waiting for transfers between devices, shards(): iterate_cols = lax.all_gather(cur_low, 'row', axis=0, tiled=True)  249 us
    all_gather x1, waiting for transfers between devices, shards(): panel_cols = lax.all_gather(mat_low, 'row', axis=0, tiled=True)  118 us
    all_gather x3, waiting for transfers between devices, shards(): lax.all_gather(shift_low, 'col', axis=1, tiled=True)  102 us
    psum x2, blocking collectives, shards(): summed = lax.psum(lax.psum(jnp.stack(partial_list), 'col'), 'row')  98.3 us
    all_gather x2, waiting for transfers between devices, shards(): iterate_rows = lax.all_gather(cur_low, 'col', axis=1, tiled=True)  69 us
    psum x1, blocking collectives, shards(): sq_total = lax.psum(jnp.sum(matrix * matrix), ('row', 'col'))  41 us
    dot_general x3, matrix products, shards(): jnp.dot(iterate_rows, panel_cols, preferred_element_type=jnp.float32)  36.2 us
    dot_general x3, matrix products, shards(): jnp.dot(lax.all_gather(shift_low, 'col', axis=1, tiled=True), iterate_col...  30.2 us
  transfers between devices with their start and end apart: 11, of which 8 were waited for; matrix products, arithmetic and copies ran while one was open for 1% of the time, Pallas kernels for 0%

profile of v1, /device:TPU:8, one launch (start us, length us, event | category | flops | bytes accessed | tf_op | source)
XLA Modules:
  0.0 777.6 jit_solution(14560147434031521570)
XLA Ops:
  7.2 0.0 all-gather.10.cloned.1.call-start
  7.2 4.3 multiply_reduce_fusion.3
  11.5 0.0 all-gather.10.cloned.1.call-update
  11.5 0.0 all-gather.12.cloned.1.call-start
  11.5 0.7 all-gather.12.cloned.1.call-update
  12.3 0.0 all-gather.14.cloned.1.call-start
  12.3 41.0 %psum.21 = f32[]{:T(128)} all-reduce(f32[]{:T(128)} %get-tuple-element.9), channel_id=1, replica_groups=mesh['row'=8,'col'=4] {'row','col'}, use_global_device_ids=true, to_apply=%region_1.0 | all-reduce | flops 1 | bytes 8 | tf_op jit(solution)/shard_map/psum | solution.py:52
  54.5 118.4 %all-gather.12.cloned.1.call-done = bf16[4096,1024]{1,0:T(8,128)(2,1)} async-done(((bf16[512,1024]{1,0:T(8,128)(2,1)}), bf16[4096,1024]{1,0:T(8,128)(2,1)}) %all-gather.12.cloned.1.call-update) | async-done | bytes 8388624 | tf_op jit(solution)/shard_map/all_gather | solution.py:54
  172.9 12.1 %fusion.12 = (bf16[512,1024]{1,0:T(8,128)(2,1)}, f32[512,1024]{1,0:T(8,128)}) fusion(s32[1024]{0:T(1024)S(1)} %iota_add_fusion, s32[512]{0:T(512)S(1)} %iota_add_fusion.1, bf16[4096,1024]{1,0:T(8,128)(2,1)} %all-gather.12.cloned.1.call-done, bf16[512,4096]{1,0:T(8,128)(2,1)} %all-gather.10.cloned.1.call-done, f32[]{:T(128)} %reduce_precision.12), kind=kOutput, calls=%fused_computation.21 | convolution fusion | flops 4316463104 | bytes 15734788 | tf_op jit(solution)/shard_map/dot_general | solution.py:62
  185.0 0.0 all-gather.14.cloned.1.call-update
  185.1 0.0 all-gather.16.cloned.1.call-start
  185.1 34.6 %all-gather.14.cloned.1.call-done = bf16[512,4096]{1,0:T(8,128)(2,1)} async-done(((bf16[512,1024]{1,0:T(8,128)(2,1)}), bf16[512,4096]{1,0:T(8,128)(2,1)}) %all-gather.14.cloned.1.call-update) | async-done | bytes 4194320 | tf_op jit(solution)/shard_map/all_gather | solution.py:67
  219.7 11.9 %fusion.17 = bf16[512,1024]{1,0:T(8,128)(2,1)} fusion(bf16[512,4096]{1,0:T(8,128)(2,1)} %all-gather.14.cloned.1.call-done, bf16[4096,1024]{1,0:T(8,128)(2,1)} %all-gather.12.cloned.1.call-done, s32[1024]{0:T(1024)S(1)} %iota_add_fusion, f32[]{:T(128)} %reduce_precision.12), kind=kOutput, calls=%fused_computation.30 | convolution fusion | flops 4333240320 | bytes 13635588 | tf_op jit(solution)/shard_map/dot_general | solution.py:66
  231.7 0.0 all-gather.16.cloned.1.call-update
  231.7 0.2 all-gather.18.cloned.1.call-start
  231.9 34.4 %all-gather.16.cloned.1.call-done = bf16[512,4096]{1,0:T(8,128)(2,1)} async-done(((bf16[512,1024]{1,0:T(8,128)(2,1)}), bf16[512,4096]{1,0:T(8,128)(2,1)}) %all-gather.16.cloned.1.call-update) | async-done | bytes 4194320 | tf_op jit(solution)/shard_map/all_gather | solution.py:73
  266.3 10.9 %fusion.13 = (bf16[512,1024]{1,0:T(8,128)(2,1)}, f32[512,1024]{1,0:T(8,128)}) fusion(s32[1024]{0:T(1024)S(1)} %iota_add_fusion, s32[512]{0:T(512)S(1)} %iota_add_fusion.1, bf16[512,4096]{1,0:T(8,128)(2,1)} %all-gather.16.cloned.1.call-done, bf16[4096,1024]{1,0:T(8,128)(2,1)} %all-gather.12.cloned.1.call-done), kind=kOutput, calls=%fused_computation.22 | convolution fusion | flops 4297588736 | bytes 15734784 | tf_op jit(solution)/shard_map/dot_general | solution.py:62
  277.2 0.0 all-gather.18.cloned.1.call-update
  277.2 0.0 all-gather.20.cloned.1.call-start
  277.2 0.5 all-gather.20.cloned.1.call-update
  277.8 0.0 copy-start.1
  277.8 0.0 all-gather.22.cloned.1.call-start
  277.8 34.0 %all-gather.18.cloned.1.call-done = bf16[512,4096]{1,0:T(8,128)(2,1)} async-done(((bf16[512,1024]{1,0:T(8,128)(2,1)}), bf16[512,4096]{1,0:T(8,128)(2,1)}) %all-gather.18.cloned.1.call-update) | async-done | bytes 4194320 | tf_op jit(solution)/shard_map/all_gather | solution.py:67
  311.8 124.6 %all-gather.20.cloned.1.call-done = bf16[4096,1024]{1,0:T(8,128)(2,1)} async-done(((bf16[512,1024]{1,0:T(8,128)(2,1)}), bf16[4096,1024]{1,0:T(8,128)(2,1)}) %all-gather.20.cloned.1.call-update) | async-done | bytes 8388624 | tf_op jit(solution)/shard_map/all_gather | solution.py:74
  436.4 10.1 %convolution_convert_fusion = bf16[512,1024]{1,0:T(8,128)(2,1)} fusion(bf16[512,4096]{1,0:T(8,128)(2,1)} %all-gather.18.cloned.1.call-done, bf16[4096,1024]{1,0:T(8,128)(2,1)} %all-gather.20.cloned.1.call-done), kind=kOutput, calls=%fused_computation.31 | convolution fusion | flops 4295491584 | bytes 13631488 | tf_op jit(solution)/shard_map/dot_general | solution.py:66
  446.6 0.0 all-gather.22.cloned.1.call-update
  446.6 0.0 all-gather.24.cloned.1.call-start
  446.6 34.6 %all-gather.22.cloned.1.call-done = bf16[512,4096]{1,0:T(8,128)(2,1)} async-done(((bf16[512,1024]{1,0:T(8,128)(2,1)}), bf16[512,4096]{1,0:T(8,128)(2,1)}) %all-gather.22.cloned.1.call-update) | async-done | bytes 4194320 | tf_op jit(solution)/shard_map/all_gather | solution.py:73
  481.2 13.2 %fusion.16 = (f32[]{:T(128)}, f32[]{:T(128)}, f32[]{:T(128)}, f32[]{:T(128)}, bf16[512,1024]{1,0:T(8,128)(2,1)}) fusion(f32[512,1024]{1,0:T(8,128)S(1)} %copy-done.1, f32[]{:T(128)} %reduce_precision.12, s32[1024]{0:T(1024)S(1)} %iota_add_fusion, s32[512]{0:T(512)S(1)} %iota_add_fusion.1, f32[512,1024]{1,0:T(8,128)} %get-tuple-element.14, ...), kind=kOutput, calls=%fused_computation.25 | convolution fusion | flops 4304404480 | bytes 19929108 | tf_op jit(solution)/shard_map/dot_general | solution.py:62
  494.4 0.0 all-gather.24.cloned.1.call-update
  494.4 0.3 all-gather.26.cloned.1.call-start
  494.7 0.5 all-gather.26.cloned.1.call-update
  495.2 33.9 %all-gather.24.cloned.1.call-done = bf16[512,4096]{1,0:T(8,128)(2,1)} async-done(((bf16[512,1024]{1,0:T(8,128)(2,1)}), bf16[512,4096]{1,0:T(8,128)(2,1)}) %all-gather.24.cloned.1.call-update) | async-done | bytes 4194320 | tf_op jit(solution)/shard_map/all_gather | solution.py:67
  529.0 124.8 %all-gather.26.cloned.1.call-done = bf16[4096,1024]{1,0:T(8,128)(2,1)} async-done(((bf16[512,1024]{1,0:T(8,128)(2,1)}), bf16[4096,1024]{1,0:T(8,128)(2,1)}) %all-gather.26.cloned.1.call-update) | async-done | bytes 8388624 | tf_op jit(solution)/shard_map/all_gather | solution.py:74
  653.8 8.1 %fusion.20 = f32[512,1024]{1,0:T(8,128)S(1)} fusion(bf16[512,4096]{1,0:T(8,128)(2,1)} %all-gather.24.cloned.1.call-done, bf16[4096,1024]{1,0:T(8,128)(2,1)} %all-gather.26.cloned.1.call-done), kind=kOutput, calls=%fused_computation.40 | convolution fusion | flops 4294967296 | bytes 14680064 | tf_op jit(solution)/shard_map/dot_general | solution.py:66
  662.0 0.2 constant_dynamic-slice_fusion
  662.2 3.0 collective-permute-start
  665.2 0.7 collective-permute-start.1
  665.9 2.6 pad_maximum_fusion
  668.5 7.8 %psum.22 = f32[4]{0:T(128)S(1)} all-reduce(f32[4]{0:T(128)S(1)} %pad_maximum_fusion), channel_id=1, replica_groups=mesh['row'=8,'col'=4] {'col'}, use_global_device_ids=true, to_apply=%region_6.0 | all-reduce | flops 4 | bytes 32 | tf_op jit(solution)/shard_map/psum | solution.py:75
  676.3 90.5 %psum.23 = f32[4]{0:T(128)S(1)} all-reduce(f32[4]{0:T(128)S(1)} %psum.22), channel_id=1, replica_groups=mesh['row'=8,'col'=4] {'row'}, use_global_device_ids=true, to_apply=%region_7.0 | all-reduce | flops 4 | bytes 32 | tf_op jit(solution)/shard_map/psum | solution.py:75
  766.8 0.5 multiply_sqrt_fusion
  767.3 1.6 copy.3
  768.9 0.3 copy.4
  769.2 0.2 broadcast_in_dim.3
  769.5 0.1 constant_dynamic-update-slice_fusion.1
  769.6 0.1 constant_dynamic-update-slice_fusion
  769.7 1.3 copy-done
  (7 shorter events, 0.0 us)
Async XLA Ops:
  7.2 47.3 %all-gather.10.cloned.1.call-start = ((), (), s32[]{:S(2)}) async-start(), calls=%async_computation | async-start | bytes 5242880 | tf_op jit(solution)/shard_map/all_gather | solution.py:53
  11.5 161.4 %all-gather.12.cloned.1.call-start = ((), (), s32[]{:S(2)}) async-start(), calls=%async_computation.1 | async-start | bytes 9437184 | tf_op jit(solution)/shard_map/all_gather | solution.py:54
  12.3 207.5 %all-gather.14.cloned.1.call-start = ((), (), s32[]{:S(2)}) async-start(), calls=%async_computation.2 | async-start | bytes 5242880 | tf_op jit(solution)/shard_map/all_gather | solution.py:67
  185.1 81.2 %all-gather.16.cloned.1.call-start = ((), (), s32[]{:S(2)}) async-start(), calls=%async_computation.3 | async-start | bytes 5242880 | tf_op jit(solution)/shard_map/all_gather | solution.py:73
  231.7 80.1 %all-gather.18.cloned.1.call-start = ((), (), s32[]{:S(2)}) async-start(), calls=%async_computation.4 | async-start | bytes 5242880 | tf_op jit(solution)/shard_map/all_gather | solution.py:67
  277.2 159.3 %all-gather.20.cloned.1.call-start = ((), (), s32[]{:S(2)}) async-start(), calls=%async_computation.5 | async-start | bytes 9437184 | tf_op jit(solution)/shard_map/all_gather | solution.py:74
  277.8 203.5 %copy-start.1 = (f32[512,1024]{1,0:T(8,128)S(1)}, f32[512,1024]{1,0:T(8,128)}, u32[]{:S(2)}) copy-start(f32[512,1024]{1,0:T(8,128)} %param.1) | copy-start | bytes 6291460
  277.8 203.5 %all-gather.22.cloned.1.call-start = ((), (), s32[]{:S(2)}) async-start(), calls=%async_computation.6 | async-start | bytes 5242880 | tf_op jit(solution)/shard_map/all_gather | solution.py:73
  446.6 82.4 %all-gather.24.cloned.1.call-start = ((), (), s32[]{:S(2)}) async-start(), calls=%async_computation.7 | async-start | bytes 5242880 | tf_op jit(solution)/shard_map/all_gather | solution.py:67
  494.4 159.4 %all-gather.26.cloned.1.call-start = ((), (), s32[]{:S(2)}) async-start(), calls=%async_computation.8 | async-start | bytes 9437184 | tf_op jit(solution)/shard_map/all_gather | solution.py:74
  662.2 105.1 %collective-permute-start = (f32[512,512]{1,0:T(8,128)S(1)}, f32[512,512]{1,0:T(8,128)}, u32[]{:S(2)}, u32[]{:S(2)}) collective-permute-start(f32[512,512]{1,0:T(8,128)S(1)} %get-tuple-element.8), channel_id=1, source_target_pairs={{0,0},{1,8},{2,16},{3,24},{4,4},{5,12},{6,20},{7,28},{8,1},{9,9},{... | collective-permute-start | bytes 3145736 | tf_op jit(solution)/shard_map/ppermute | solution.py:34
  665.2 103.7 %collective-permute-start.1 = (f32[512,512]{1,0:T(8,128)S(1)}, f32[512,512]{1,0:T(8,128)S(1)}, u32[]{:S(2)}, u32[]{:S(2)}) collective-permute-start(f32[512,512]{1,0:T(8,128)S(1)} %get-tuple-element.7), channel_id=1, source_target_pairs={{0,4},{1,12},{2,20},{3,28},{4,0},{5,8},{6,16},{7,24},{8,5},{9,13},... | collective-permute-start | bytes 3145736 | tf_op jit(solution)/shard_map/ppermute | solution.py:34
  769.7 1.3 copy-start
Sparse Core Ops, SparseCore 0:
  11.6 35.8 all-gather.9
  50.2 122.6 all-gather.11
  185.2 34.4 all-gather.13
  231.8 34.4 all-gather.15
  277.3 34.4 all-gather.17
  313.8 122.6 all-gather.19
  446.7 34.4 all-gather.21
  494.5 34.4 all-gather.23
  531.2 122.6 all-gather.25
